TPU v7x, 128 devices: a whole 4x4x4 slice. The times are simulated.
128 devices in a mesh: dp: 32 (over y, z, core), fsdp: 4 (over x).
Axes of the slice: x: 4, y: 4, z: 4, core: 2. Of those that a mesh axis runs over, the one named last changes fastest.
Arguments:
- tokens: bfloat16 [65536, 4096], P(('dp', 'fsdp')), may hold values from -0.75 to 0.75
- doc_ids: int32 [65536], P(('dp', 'fsdp')), may hold values from 0 to 63, never falling along the last dimension, each value on 1 to 2048 neighbouring positions
- attn_gain: float32 [4096], replicated, may hold values from 0.1 to 1.9
- mlp_gain: float32 [4096], replicated, may hold values from 0.1 to 1.9
- w_query: bfloat16 [4096, 512], P(('dp', 'fsdp')), may hold values from -1 to 1
- w_key_value: bfloat16 [4096, 256], P(('dp', 'fsdp')), may hold values from -3 to 3
- w_out: bfloat16 [512, 4096], P(None, ('dp', 'fsdp')), may hold values from -0.25 to 0.25
- w_gate: bfloat16 [4096, 1024], P(('dp', 'fsdp')), may hold values from -0.09375 to 0.09375
- w_up: bfloat16 [4096, 1024], P(('dp', 'fsdp')), may hold values from -0.09375 to 0.09375
- w_down: bfloat16 [1024, 4096], P(None, ('dp', 'fsdp')), may hold values from -0.1875 to 0.1875
Outputs:
- mixed: bfloat16 [65536, 4096], P(('dp', 'fsdp'))
Inputs may be any that keep to these rules, and one draw needn't show every extreme that they name: `doc_ids`: document numbers never fall along the pack, and every document has at most 2048 tokens.
All inputs are finite; a program needn't handle non-finite values.
Results may differ from a plain program's by a relative error of at most 0.02.
The roundings to bfloat16 on the way count: a program that leaves them out, or rounds other values in their place, can miss the bound.
Values may be sent and summed in bfloat16 or wider, within the bound.
A program may use at most 128 MiB of HBM per device.

v0:
```python
import math

import jax
import jax.numpy as jnp
from jax import lax
from jax.sharding import PartitionSpec as P

SPAN = 4


EPS = 1e-05
THETA = 500000.0
NEGATIVE = -1e30


def sent_together(arrays, axis, dim, along):
    widths = [a.shape[along] for a in arrays]
    both = jnp.concatenate(arrays, axis=along)
    out = lax.all_gather(both, axis, axis=dim, tiled=True)
    return tuple(jnp.split(out, [sum(widths[:k]) for k in range(1, len(widths))], axis=along))


def shifted(array, axis, by):
    length = lax.axis_size(axis)
    pairs = [(i, i + by) for i in range(length) if 0 <= i + by < length]
    return lax.ppermute(array, axis, pairs)


def rms_scale(values, gain):
    wide = values.astype(jnp.float32)
    power = jnp.mean(wide * wide, axis=-1, keepdims=True)
    return (wide * lax.rsqrt(power + EPS) * gain).astype(jnp.bfloat16)


def rotate(values, position):
    head = values.shape[-1]
    half = head // 2
    freqs = THETA ** (-2.0 * jnp.arange(half, dtype=jnp.float32) / head)
    angle = position.astype(jnp.float32)[:, None, None] * freqs[None, None, :]
    cosine = jnp.cos(angle)
    sine = jnp.sin(angle)
    first = values[..., :half]
    second = values[..., half:]
    return jnp.concatenate(
        [first * cosine - second * sine, second * cosine + first * sine], axis=-1
    )


def head_scores(query, keys):
    return jnp.einsum("qhd,kd->hqk", query, keys, preferred_element_type=jnp.float32) / math.sqrt(
        query.shape[-1]
    )


def weigh_values(weights, values):
    return jnp.einsum(
        "hqk,kd->qhd", weights.astype(jnp.bfloat16), values, preferred_element_type=jnp.float32
    )


def attend_live(query, halo_pairs, halo_marks, own_pairs, marks, block):
    head = query.shape[-1]
    index = jnp.arange(query.shape[0], dtype=jnp.int32)
    allowed = (marks[None, :] == marks[:, None]) & (index[None, :] <= index[:, None])
    own_scores = jnp.where(allowed[None, :, :], head_scores(query, own_pairs[:, :head]), NEGATIVE)
    count = halo_marks.shape[0] // block
    live = jnp.sum(jnp.any(halo_marks.reshape(count, block) == marks[0], axis=1).astype(jnp.int32))
    peak = jnp.max(own_scores, axis=2)
    weights = jnp.exp(own_scores - peak[:, :, None])
    totals = jnp.sum(weights, axis=2)
    mixed = weigh_values(weights, own_pairs[:, head:])

    def add_block(step, carry):
        old_peak, old_totals, old_mixed = carry
        begin = (count - 1 - step) * block
        pairs = lax.dynamic_slice_in_dim(halo_pairs, begin, block, 0)
        block_marks = lax.dynamic_slice_in_dim(halo_marks, begin, block, 0)
        same = (block_marks[None, :] == marks[:, None])[None, :, :]
        scores = jnp.where(same, head_scores(query, pairs[:, :head]), NEGATIVE)
        new_peak = jnp.maximum(old_peak, jnp.max(scores, axis=2))
        factor = jnp.exp(old_peak - new_peak)
        block_weights = jnp.exp(scores - new_peak[:, :, None])
        new_totals = old_totals * factor + jnp.sum(block_weights, axis=2)
        new_mixed = old_mixed * jnp.transpose(factor)[:, :, None] + weigh_values(
            block_weights, pairs[:, head:]
        )
        return (new_peak, new_totals, new_mixed)

    peak, totals, mixed = lax.fori_loop(0, live, add_block, (peak, totals, mixed))
    return mixed / jnp.transpose(totals)[:, :, None]


def per_device(
    tokens, doc_ids, attn_gain, mlp_gain, w_query, w_key_value, w_out, w_gate, w_up, w_down
):
    rows = tokens.shape[0]
    rank = lax.axis_index(("dp", "fsdp"))
    normed = rms_scale(tokens, attn_gain)
    query_width = w_query.shape[1]
    pair_width = w_key_value.shape[1]
    head = pair_width // 2
    heads = query_width // head
    group_query, group_pair = sent_together((w_query, w_key_value), "fsdp", 0, 1)
    pieces = sent_together((group_query, group_pair), "dp", 0, 1)
    columns = normed
    query_raw = jnp.dot(columns, pieces[0], preferred_element_type=jnp.float32)
    pair_raw = jnp.dot(columns, pieces[1], preferred_element_type=jnp.float32)
    position = rank * rows + jnp.arange(rows, dtype=jnp.int32)
    query = rotate(query_raw.reshape(rows, heads, head), position).astype(jnp.bfloat16)
    keys = rotate(pair_raw[:, None, :head], position)[:, 0, :].astype(jnp.bfloat16)
    values = pair_raw[:, head:].astype(jnp.bfloat16)
    own_pairs = jnp.concatenate([keys, values], axis=1)
    marks = doc_ids + 1
    pair_pieces = []
    mark_pieces = []
    for distance in range(SPAN, 0, -1):
        moved_pairs, moved_marks = shifted((own_pairs, marks), ("dp", "fsdp"), distance)
        pair_pieces.append(moved_pairs)
        mark_pieces.append(moved_marks)
    halo_pairs = jnp.concatenate(pair_pieces, axis=0)
    halo_marks = jnp.concatenate(mark_pieces, axis=0)
    mixed = attend_live(query, halo_pairs, halo_marks, own_pairs, marks, rows)
    attended = mixed.reshape(rows, query_width).astype(jnp.bfloat16)
    projected = jnp.dot(
        attended,
        lax.all_gather(w_out, ("dp", "fsdp"), axis=1, tiled=True),
        preferred_element_type=jnp.float32,
    )
    resid = (tokens.astype(jnp.float32) + projected).astype(jnp.bfloat16)
    resid = lax.optimization_barrier(resid)
    normed_mlp = rms_scale(resid, mlp_gain)
    group_gate, group_up = sent_together((w_gate, w_up), "fsdp", 0, 1)
    pieces = sent_together((group_gate, group_up), "dp", 0, 1)
    columns = normed_mlp
    gate = jnp.dot(columns, pieces[0], preferred_element_type=jnp.float32)
    up_value = jnp.dot(columns, pieces[1], preferred_element_type=jnp.float32)
    hidden = (jax.nn.silu(gate) * up_value).astype(jnp.bfloat16)
    down = jnp.dot(
        hidden,
        lax.all_gather(w_down, ("dp", "fsdp"), axis=1, tiled=True),
        preferred_element_type=jnp.float32,
    )
    return (resid.astype(jnp.float32) + down).astype(jnp.bfloat16)


def solution(mesh):
    in_specs = (
        P(("dp", "fsdp"), None),
        P(("dp", "fsdp")),
        P(),
        P(),
        P(("dp", "fsdp"), None),
        P(("dp", "fsdp"), None),
        P(None, ("dp", "fsdp")),
        P(("dp", "fsdp"), None),
        P(("dp", "fsdp"), None),
        P(None, ("dp", "fsdp")),
    )
    out_specs = P(("dp", "fsdp"), None)
    return jax.shard_map(
        per_device, mesh=mesh, in_specs=in_specs, out_specs=out_specs, check_vma=False
    )
```

profile of v0, /device:TPU:1, one launch (start us, length us, event | category | flops | bytes accessed | tf_op | source)
XLA Modules:
  0.0 306.7 jit_solution(3767838602492783908)
XLA Ops:
  7.3 11.6 %all_gather.18 = bf16[128,768]{1,0:T(8,128)(2,1)} all-gather(bf16[32,768]{1,0:T(8,128)(2,1)S(1)} %pad_maximum_fusion.6), channel_id=1, replica_groups=mesh['dp'=32,'fsdp'=4] {'fsdp'}, dimensions={0}, use_global_device_ids=true | all-gather | bytes 245760 | tf_op jit(solution)/shard_map/all_gather | solution.py:19
  20.6 10.6 %all_gather.21 = bf16[128,2048]{1,0:T(8,128)(2,1)} all-gather(bf16[32,2048]{1,0:T(8,128)(2,1)S(1)} %pad_maximum_fusion.4), channel_id=1, replica_groups=mesh['dp'=32,'fsdp'=4] {'fsdp'}, dimensions={0}, use_global_device_ids=true | all-gather | bytes 655360 | tf_op jit(solution)/shard_map/all_gather | solution.py:19
  32.0 9.7 %collective-permute-start = (s32[512]{0:T(512)S(1)}, s32[512]{0:T(512)S(1)}, u32[]{:S(2)}, u32[]{:S(2)}) collective-permute-start(s32[512]{0:T(512)S(1)} %broadcast_add_fusion), channel_id=1, source_target_pairs={{0,4},{1,5},{2,6},{3,7},{4,8},{5,9},{6,10},{7,11},{8,12},{9,13},{1... | collective-permute-start | bytes 6152 | tf_op jit(solution)/shard_map/ppermute | solution.py:26
  41.7 3.9 %collective-permute-start.1 = (s32[512]{0:T(512)S(1)}, s32[512]{0:T(512)S(1)}, u32[]{:S(2)}, u32[]{:S(2)}) collective-permute-start(s32[512]{0:T(512)S(1)} %broadcast_add_fusion), channel_id=1, source_target_pairs={{0,3},{1,4},{2,5},{3,6},{4,7},{5,8},{6,9},{7,10},{8,11},{9,12},{10... | collective-permute-start | bytes 6152 | tf_op jit(solution)/shard_map/ppermute | solution.py:26
  50.3 3.1 %fusion.17 = f32[512]{0:T(512)S(1)} fusion(bf16[512,4096]{1,0:T(8,128)(2,1)} %param.12), kind=kLoop, calls=%fused_computation.25 | loop fusion | flops 6290944 | bytes 4196352 | tf_op jit(solution)/shard_map/reduce_sum | solution.py:31
  56.5 16.5 %all-gather.5.cloned.1.call-done = bf16[4096,768]{1,0:T(8,128)(2,1)} async-done(((bf16[128,768]{1,0:T(8,128)(2,1)}), bf16[4096,768]{1,0:T(8,128)(2,1)}) %all-gather.5.cloned.1.call-update) | async-done | bytes 6291472 | tf_op jit(solution)/shard_map/all_gather | solution.py:19
  73.0 4.6 %fusion.34 = f32[512,256]{0,1:T(8,128)S(1)} fusion(bf16[4096,768]{1,0:T(8,128)(2,1)} %all-gather.5.cloned.1.call-done, bf16[512,4096]{1,0:T(8,128)(2,1)} %param.12, f32[4096]{0:T(1024)S(1)} %copy-done.8, f32[512]{0:T(512)S(1)} %add_rsqrt_fusion.1), kind=kOutput, calls=%fused_computation.44 | convolution fusion | flops 1082130432 | bytes 6834176 | tf_op jit(solution)/shard_map/dot_general | solution.py:107
  79.0 2.3 collective-permute-start.4
  81.3 4.3 %collective-permute-start.5 = (bf16[512,256]{0,1:T(8,128)(2,1)}, bf16[512,256]{0,1:T(8,128)(2,1)}, u32[]{:S(2)}, u32[]{:S(2)}) collective-permute-start(bf16[512,256]{0,1:T(8,128)(2,1)} %pad_maximum_fusion.2), channel_id=1, source_target_pairs={{0,3},{1,4},{2,5},{3,6},{4,7},{5,8},{6,9},{7,10},{8,11},{9,12},{10... | collective-permute-start | bytes 786440 | tf_op jit(solution)/shard_map/ppermute | solution.py:26
  85.6 2.4 collective-permute-start.6
  88.0 2.6 collective-permute-start.7
  90.7 2.6 fusion.29
  98.0 5.3 %collective-permute-done.7 = bf16[512,256]{0,1:T(8,128)(2,1)} collective-permute-done((bf16[512,256]{0,1:T(8,128)(2,1)}, bf16[512,256]{0,1:T(8,128)(2,1)}, u32[]{:S(2)}, u32[]{:S(2)}) %collective-permute-start.7) | collective-permute-done | bytes 262176 | tf_op jit(solution)/shard_map/ppermute | solution.py:26
  104.7 9.5 %while.14 = (s32[]{:T(128)}, f32[4,512]{1,0:T(4,128)S(1)}, f32[4,512]{1,0:T(4,128)S(1)}, f32[512,4,128]{0,2,1:T(8,128)S(1)}, s32[]{:T(128)}, /*index=5*/s32[2048...) while((s32[]{:T(128)}, f32[4,512]{1,0:T(4,128)S(1)}, ...), condition=%wide.region_8.9_spmd, body=%wide.region_5.8_spmd.sunk | while | flops 549197824 | bytes 33431808 | solution.py:89
  105.6 2.9 fusion.80
  108.5 3.8 %fusion.83 = f32[512,4,128]{0,2,1:T(8,128)S(1)} fusion(f32[512,512,4]{1,0,2:T(8,128)} %get-tuple-element.168, f32[4,512]{1,0:T(4,128)S(1)} %get-tuple-element.201, pred[512,512]{0,1:T(8,128)(4,1)S(1)} %broadcast_compare_fusion.3, f32[512,4,128]{0,2,1:T(8,128)S(1)} %get-tuple-element.188, f32[512,4]{0,1:T(4,128)S(1)} %get-tuple-element.169, ...), kind=kOutput, calls=%fused_computation.8.clone.1 | convolution fusion | flops 273154048 | bytes 6701064 | tf_op jit(solution)/shard_map/while/body/hqk,kd->qhd/dot_general | solution.py:56
  114.3 30.9 %all-gather.7.cloned.1.call-done = bf16[512,4096]{0,1:T(8,128)(2,1)} async-done(((bf16[512,32]{0,1:T(8,128)(2,1)}), bf16[512,4096]{0,1:T(8,128)(2,1)}) %all-gather.7.cloned.1.call-update) | async-done | bytes 4194320 | tf_op jit(solution)/shard_map/all_gather | solution.py:126
  145.2 5.9 %fusion.20 = bf16[512,4096]{1,0:T(8,128)(2,1)S(1)} fusion(bf16[512,4096]{1,0:T(8,128)(2,1)} %param.12, bf16[512,512]{0,1:T(8,128)(2,1)S(1)} %bitcast.82, bf16[512,4096]{0,1:T(8,128)(2,1)} %all-gather.7.cloned.1.call-done), kind=kOutput, calls=%fused_computation.28 | convolution fusion | flops 2153775104 | bytes 13107200 | tf_op jit(solution)/shard_map/dot_general | solution.py:124
  154.0 63.8 %all-gather.9.cloned.1.call-done = bf16[4096,2048]{1,0:T(8,128)(2,1)} async-done(((bf16[128,2048]{1,0:T(8,128)(2,1)}), bf16[4096,2048]{1,0:T(8,128)(2,1)}) %all-gather.9.cloned.1.call-update) | async-done | bytes 16777232 | tf_op jit(solution)/shard_map/all_gather | solution.py:19
  217.8 8.4 %fusion.27 = f32[512,1024]{1,0:T(8,128)S(1)} fusion(bf16[4096,2048]{1,0:T(8,128)(2,1)} %all-gather.9.cloned.1.call-done, bf16[512,4096]{1,0:T(8,128)(2,1)} %copy-done.2, f32[4096]{0:T(1024)S(1)} %copy-done.9, f32[512]{0:T(512)S(1)} %add_rsqrt_fusion), kind=kOutput, calls=%fused_computation.35 | convolution fusion | flops 4303355904 | bytes 14698496 | tf_op jit(solution)/shard_map/dot_general | solution.py:135
  226.3 2.3 copy-done.6
  228.6 4.7 %multiply_convert_fusion = bf16[512,1024]{1,0:T(8,128)(2,1)S(1)} fusion(f32[512,1024]{1,0:T(8,128)S(1)} %fusion.27, bf16[4096,2048]{1,0:T(8,128)(2,1)S(1)} %copy-done.6, bf16[512,4096]{1,0:T(8,128)(2,1)S(1)} %copy-done.3, f32[4096]{0:T(1024)S(1)} %copy-done.9, f32[512]{0:T(512)S(1)} %add_rsqrt_fusion), kind=kOutput, calls=%fused_computation.46 | convolution fusion | flops 4306501632 | bytes 15747072 | tf_op jit(solution)/shard_map/dot_general | solution.py:136
  233.3 56.6 %all-gather.11.cloned.1.call-done = bf16[1024,4096]{0,1:T(8,128)(2,1)} async-done(((bf16[1024,32]{0,1:T(8,128)(2,1)}), bf16[1024,4096]{0,1:T(8,128)(2,1)}) %all-gather.11.cloned.1.call-update) | async-done | bytes 8388624 | tf_op jit(solution)/shard_map/all_gather | solution.py:140
  289.9 10.2 %fusion.24 = bf16[512,4096]{1,0:T(8,128)(2,1)} fusion(bf16[512,4096]{1,0:T(8,128)(2,1)} %copy-done.2, bf16[512,1024]{1,0:T(8,128)(2,1)S(1)} %multiply_convert_fusion, bf16[1024,4096]{0,1:T(8,128)(2,1)} %all-gather.11.cloned.1.call-done), kind=kOutput, calls=%fused_computation.32 | convolution fusion | flops 4301258752 | bytes 17825792 | tf_op jit(solution)/shard_map/dot_general | solution.py:138
  (77 shorter events, 22.5 us)
Async XLA Ops:
  6.5 66.5 %copy-start.8 = (f32[4096]{0:T(1024)S(1)}, f32[4096]{0:T(1024)}, u32[]{:S(2)}) copy-start(f32[4096]{0:T(1024)} %param.14) | copy-start | bytes 49156
  6.5 66.5 %all-gather.5.cloned.1.call-start = ((), (), s32[]{:S(2)}) async-start(), calls=%async_computation | async-start | bytes 6488064 | tf_op jit(solution)/shard_map/all_gather | solution.py:19
  18.9 126.3 %all-gather.7.cloned.1.call-start = ((), (), s32[]{:S(2)}) async-start(), calls=%async_computation.1 | async-start | bytes 4227072 | tf_op jit(solution)/shard_map/all_gather | solution.py:126
  19.7 198.2 %all-gather.9.cloned.1.call-start = ((), (), s32[]{:S(2)}) async-start(), calls=%async_computation.2 | async-start | bytes 17301504 | tf_op jit(solution)/shard_map/all_gather | solution.py:19
  31.3 258.7 %all-gather.11.cloned.1.call-start = ((), (), s32[]{:S(2)}) async-start(), calls=%async_computation.3 | async-start | bytes 8454144 | tf_op jit(solution)/shard_map/all_gather | solution.py:140
  32.0 22.9 %collective-permute-start = (s32[512]{0:T(512)S(1)}, s32[512]{0:T(512)S(1)}, u32[]{:S(2)}, u32[]{:S(2)}) collective-permute-start(s32[512]{0:T(512)S(1)} %broadcast_add_fusion), channel_id=1, source_target_pairs={{0,4},{1,5},{2,6},{3,7},{4,8},{5,9},{6,10},{7,11},{8,12},{9,13},{1... | collective-permute-start | bytes 6152 | tf_op jit(solution)/shard_map/ppermute | solution.py:26
  41.7 13.2 %collective-permute-start.1 = (s32[512]{0:T(512)S(1)}, s32[512]{0:T(512)S(1)}, u32[]{:S(2)}, u32[]{:S(2)}) collective-permute-start(s32[512]{0:T(512)S(1)} %broadcast_add_fusion), channel_id=1, source_target_pairs={{0,3},{1,4},{2,5},{3,6},{4,7},{5,8},{6,9},{7,10},{8,11},{9,12},{10... | collective-permute-start | bytes 6152 | tf_op jit(solution)/shard_map/ppermute | solution.py:26
  45.6 9.3 %collective-permute-start.2 = (s32[512]{0:T(512)S(1)}, s32[512]{0:T(512)S(1)}, u32[]{:S(2)}, u32[]{:S(2)}) collective-permute-start(s32[512]{0:T(512)S(1)} %broadcast_add_fusion), channel_id=1, source_target_pairs={{0,2},{1,3},{2,4},{3,5},{4,6},{5,7},{6,8},{7,9},{8,10},{9,11},{10,... | collective-permute-start | bytes 6152 | tf_op jit(solution)/shard_map/ppermute | solution.py:26
  47.8 7.1 %collective-permute-start.3 = (s32[512]{0:T(512)S(1)}, s32[512]{0:T(512)S(1)}, u32[]{:S(2)}, u32[]{:S(2)}) collective-permute-start(s32[512]{0:T(512)S(1)} %broadcast_add_fusion), channel_id=1, source_target_pairs={{0,1},{1,2},{2,3},{3,4},{4,5},{5,6},{6,7},{7,8},{8,9},{9,10},{10,1... | collective-permute-start | bytes 6152 | tf_op jit(solution)/shard_map/ppermute | solution.py:26
  73.0 17.6 %copy-start.1 = (bf16[512,4096]{1,0:T(8,128)(2,1)S(1)}, bf16[512,4096]{1,0:T(8,128)(2,1)}, u32[]{:S(2)}) copy-start(bf16[512,4096]{1,0:T(8,128)(2,1)} %param.12) | copy-start | bytes 12582916
  73.0 17.7 %copy-start.7 = (bf16[4096,768]{1,0:T(8,128)(2,1)S(1)}, bf16[4096,768]{1,0:T(8,128)(2,1)}, u32[]{:S(2)}) copy-start(bf16[4096,768]{1,0:T(8,128)(2,1)} %all-gather.5.cloned.1.call-done) | copy-start | bytes 18874372
  77.6 10.4 %copy-start.4 = (f32[512,256]{0,1:T(8,128)}, f32[512,256]{0,1:T(8,128)S(1)}, u32[]{:S(2)}) copy-start(f32[512,256]{0,1:T(8,128)S(1)} %fusion.34) | copy-start | bytes 1572868
  79.0 18.9 %collective-permute-start.4 = (bf16[512,256]{0,1:T(8,128)(2,1)}, bf16[512,256]{0,1:T(8,128)(2,1)}, u32[]{:S(2)}, u32[]{:S(2)}) collective-permute-start(bf16[512,256]{0,1:T(8,128)(2,1)} %pad_maximum_fusion.2), channel_id=1, source_target_pairs={{0,4},{1,5},{2,6},{3,7},{4,8},{5,9},{6,10},{7,11},{8,12},{9,13},{1... | collective-permute-start | bytes 786440 | tf_op jit(solution)/shard_map/ppermute | solution.py:26
  81.3 16.6 %collective-permute-start.5 = (bf16[512,256]{0,1:T(8,128)(2,1)}, bf16[512,256]{0,1:T(8,128)(2,1)}, u32[]{:S(2)}, u32[]{:S(2)}) collective-permute-start(bf16[512,256]{0,1:T(8,128)(2,1)} %pad_maximum_fusion.2), channel_id=1, source_target_pairs={{0,3},{1,4},{2,5},{3,6},{4,7},{5,8},{6,9},{7,10},{8,11},{9,12},{10... | collective-permute-start | bytes 786440 | tf_op jit(solution)/shard_map/ppermute | solution.py:26
  85.6 12.5 %collective-permute-start.6 = (bf16[512,256]{0,1:T(8,128)(2,1)}, bf16[512,256]{0,1:T(8,128)(2,1)}, u32[]{:S(2)}, u32[]{:S(2)}) collective-permute-start(bf16[512,256]{0,1:T(8,128)(2,1)} %pad_maximum_fusion.2), channel_id=1, source_target_pairs={{0,2},{1,3},{2,4},{3,5},{4,6},{5,7},{6,8},{7,9},{8,10},{9,11},{10,... | collective-permute-start | bytes 786440 | tf_op jit(solution)/shard_map/ppermute | solution.py:26
  88.0 15.4 %collective-permute-start.7 = (bf16[512,256]{0,1:T(8,128)(2,1)}, bf16[512,256]{0,1:T(8,128)(2,1)}, u32[]{:S(2)}, u32[]{:S(2)}) collective-permute-start(bf16[512,256]{0,1:T(8,128)(2,1)} %pad_maximum_fusion.2), channel_id=1, source_target_pairs={{0,1},{1,2},{2,3},{3,4},{4,5},{5,6},{6,7},{7,8},{8,9},{9,10},{10,1... | collective-permute-start | bytes 786440 | tf_op jit(solution)/shard_map/ppermute | solution.py:26
  94.3 1.3 copy-start.5
  108.5 3.8 %copy-start = (f32[512,512,4]{1,0,2:T(8,128)S(1)}, f32[512,512,4]{1,0,2:T(8,128)}, u32[]{:S(2)}) copy-start(f32[512,512,4]{1,0,2:T(8,128)} %get-tuple-element.168) | copy-start | bytes 12582916 | tf_op jit(solution)/shard_map/while
  151.1 2.0 copy-start.2
  153.1 64.7 %copy-start.9 = (f32[4096]{0:T(1024)S(1)}, f32[4096]{0:T(1024)}, u32[]{:S(2)}) copy-start(f32[4096]{0:T(1024)} %param.15) | copy-start | bytes 49156
  217.8 8.4 %copy-start.3 = (bf16[512,4096]{1,0:T(8,128)(2,1)S(1)}, bf16[512,4096]{1,0:T(8,128)(2,1)}, u32[]{:S(2)}) copy-start(bf16[512,4096]{1,0:T(8,128)(2,1)} %copy-done.2) | copy-start | bytes 12582916
  217.8 10.7 %copy-start.6 = (bf16[4096,2048]{1,0:T(8,128)(2,1)S(1)}, bf16[4096,2048]{1,0:T(8,128)(2,1)}, u32[]{:S(2)}) copy-start(bf16[4096,2048]{1,0:T(8,128)(2,1)} %all-gather.9.cloned.1.call-done) | copy-start | bytes 50331652
Sparse Core Ops, SparseCore 0:
  19.0 53.9 all-gather.4
  76.2 69.0 all-gather.6
  147.5 70.2 all-gather.8
  220.8 69.0 all-gather.10
where the time goes:
time: 307 us
  waiting for transfers between devices  174 us (57%)
  matrix products  45.4 us (15%)
  starting transfers between devices  29.8 us (10%)
  blocking collectives  22.2 us (7%)
  other arithmetic  14.4 us (5%)
  between operations  13.5 us (4%)
  local copies, waits for them, and re-layouts  5.79 us (2%)
    all_gather x2, waiting for transfers between devices, sent_together(): out = lax.all_gather(both, axis, axis=dim, tiled=True)  80.3 us
    all_gather x1, waiting for transfers between devices, per_device(): lax.all_gather(w_down, ('dp', 'fsdp'), axis=1, tiled=True)  56.6 us
    all_gather x1, waiting for transfers between devices, per_device(): lax.all_gather(w_out, ('dp', 'fsdp'), axis=1, tiled=True)  30.9 us
    ppermute x8, starting transfers between devices, shifted(): return lax.ppermute(array, axis, pairs)  29.7 us
    all_gather x2, blocking collectives, sent_together(): out = lax.all_gather(both, axis, axis=dim, tiled=True)  22.2 us
    dot_general x1, matrix products, per_device(): jnp.dot(hidden, lax.all_gather(w_down, ('dp', 'fsdp'), axis=1, tiled=True...  10.2 us
    dot_general x1, matrix products, per_device(): gate = jnp.dot(columns, pieces[0], preferred_element_type=jnp.float32)  8.4 us
  transfers between devices with their start and end apart: 12, of which 6 were waited for; matrix products, arithmetic and copies ran while one was open for 16% of the time, Pallas kernels for 0%

commit v1 on v0

v1 whole, which is shorter than its diff:
```python
import functools
import math

import jax
import jax.numpy as jnp
from jax import lax
from jax.experimental import pallas as pl
from jax.experimental.pallas import tpu as pltpu
from jax.sharding import PartitionSpec as P

MESH = pl.DeviceIdType.MESH
EPS = 1e-05
THETA = 500000.0
NEGATIVE = -1e30
SIDE = 4
SPAN = 4
GROUPS = (
    ((0, 256), (256, 256), (512, 256)),
    ((768, 128), (896, 128), (1024, 256)),
    ((1280, 640), (1920, 640), (2560, 768)),
    ((3328, 384), (3712, 384), (4096, 256)),
)
ORDERS = (("x", "y", "z"), ("y", "z", "x"), ("z", "x", "y"))
OUT_AT, GATE_AT, UP_AT, DOWN_AT, WIDTH = 768, 1280, 2304, 3328, 4352
A_AT, B_AT, C_AT, PARTNER_AT, SLOTS = 0, 3, 9, 15, 19


def kernel(
    tok, gain_attn, gain_mlp, cosine, sine, doc_row, doc_col, wq, wkv, wo, wg, wu, wd,
    out,
    w, res, nrm, qry, keys, vals, marks, att, hid,
    send, recv, halo_send, halo_recv, local_sem, tok_sem, out_sem,
):
    rows, width = res.shape
    head = qry.shape[2]
    shard = wq.shape[0]
    half = shard // 2
    dp = lax.axis_index("dp")
    x = lax.axis_index("fsdp")
    y = dp // (2 * SIDE)
    z = (dp // 2) % SIDE
    c = dp % 2
    pos = {"x": x, "y": y, "z": z}
    rank = dp * SIDE + x
    ranks = 32 * SIDE

    def device(at, core):
        return ((at["y"] * SIDE + at["z"]) * 2 + core, at["x"])

    def shift(dim, by):
        return {**pos, dim: (pos[dim] + by) % SIDE}

    def peer(dim, by):
        return device(shift(dim, by), c)

    def at_rank(by):
        other = (rank + by + ranks) % ranks
        return (other // SIDE, other % SIDE)

    local = []
    for k, (src, at) in enumerate(
        ((wq, 0), (wkv, 512), (wo, OUT_AT), (wg, GATE_AT), (wu, UP_AT), (wd, DOWN_AT))
    ):
        local.append(
            pltpu.make_async_copy(
                src, w.at[y, z, c, x, :, pl.ds(at, src.shape[1])], local_sem.at[k]
            )
        )
    for copy in local:
        copy.start()
    chunk = rows // 4
    tok_copies = [
        pltpu.make_async_copy(
            tok.at[pl.ds(k * chunk, chunk)], res.at[pl.ds(k * chunk, chunk)], tok_sem.at[k]
        )
        for k in range(4)
    ]
    for copy in tok_copies:
        copy.start()

    barrier = pltpu.get_barrier_semaphore()
    friends = [peer(dim, by) for dim in ("x", "y", "z") for by in (1, 2, 3)]
    friends.append(device(pos, 1 - c))
    friends += [at_rank(by) for by in range(-SPAN, SPAN + 1) if by != 0]
    for friend in friends:
        pl.semaphore_signal(barrier, inc=1, device_id=friend, device_id_type=MESH)
    pl.semaphore_wait(barrier, len(friends))

    sends = []

    def block(core, sel, part, r0, nr):
        at, n = part
        return w.at[
            sel["y"], sel["z"], core, sel["x"], pl.ds(r0, nr), pl.ds(at, n)
        ]

    def remote(ref, row, slot, to):
        return pltpu.make_async_remote_copy(
            src_ref=ref, dst_ref=ref, send_sem=send.at[row, slot], recv_sem=recv.at[row, slot],
            device_id=to, device_id_type=MESH,
        )

    def push(ref, row, slot, to):
        copy = remote(ref, row, slot, to)
        copy.start()
        sends.append(copy)

    ALL = slice(None)

    def each(g):
        for p in range(3):
            yield g * 3 + p, GROUPS[g][p], ORDERS[p]

    def spread(row, part, dim, base, done):
        sel = {**pos, **{d: ALL for d in done}}
        push(block(c, sel, part, 0, half), row, base + 0, peer(dim, 1))
        push(block(c, sel, part, half, half), row, base + 3, peer(dim, -1))
        push(block(c, sel, part, half, half), row, base + 1, peer(dim, 1))
        push(block(c, sel, part, 0, half), row, base + 2, peer(dim, -1))

    def relay(row, part, dim, base, done):
        back = {**shift(dim, -1), **{d: ALL for d in done}}
        ahead = {**shift(dim, 1), **{d: ALL for d in done}}
        ref = block(c, back, part, 0, half)
        remote(ref, row, base + 0, peer(dim, 1)).wait_recv()
        push(ref, row, base + 4, peer(dim, 1))
        ref = block(c, ahead, part, half, half)
        remote(ref, row, base + 3, peer(dim, 1)).wait_recv()
        push(ref, row, base + 5, peer(dim, -1))

    def near(row, part, dim, base, done):
        back = {**shift(dim, -1), **{d: ALL for d in done}}
        ahead = {**shift(dim, 1), **{d: ALL for d in done}}
        remote(block(c, back, part, half, half), row, base + 1, peer(dim, 1)).wait_recv()
        remote(block(c, ahead, part, 0, half), row, base + 2, peer(dim, 1)).wait_recv()

    def far(row, part, dim, base, done):
        across = {**shift(dim, 2), **{d: ALL for d in done}}
        remote(block(c, across, part, 0, half), row, base + 4, peer(dim, 1)).wait_recv()
        remote(block(c, across, part, half, half), row, base + 5, peer(dim, 1)).wait_recv()

    def partner_ref(core, part, order, by):
        sel = {order[0]: ALL, order[1]: ALL, order[2]: (pos[order[2]] + by) % SIDE}
        return block(core, sel, part, 0, shard)

    def to_partner(row, part, order, by):
        push(partner_ref(c, part, order, by), row, PARTNER_AT + by, device(pos, 1 - c))

    def first(g):
        for row, part, order in each(g):
            for by in (1, 3, 2):
                push(block(c, pos, part, 0, shard), row, A_AT + by - 1, peer(order[0], by))

    def second(g):
        for row, part, order in each(g):
            for by in (1, 3, 2):
                ref = block(c, shift(order[0], -by), part, 0, shard)
                remote(ref, row, A_AT + by - 1, peer(order[0], by)).wait_recv()
            spread(row, part, order[1], B_AT, order[:1])

    def second_relay(g):
        for row, part, order in each(g):
            relay(row, part, order[1], B_AT, order[:1])

    def third(g):
        for row, part, order in each(g):
            near(row, part, order[1], B_AT, order[:1])
            far(row, part, order[1], B_AT, order[:1])
            spread(row, part, order[2], C_AT, order[:2])
        for row, part, order in each(g):
            to_partner(row, part, order, 0)

    def third_relay(g):
        for row, part, order in each(g):
            relay(row, part, order[2], C_AT, order[:2])

    def third_near(g):
        for row, part, order in each(g):
            near(row, part, order[2], C_AT, order[:2])
            to_partner(row, part, order, 1)
            to_partner(row, part, order, 3)

    def third_far(g):
        for row, part, order in each(g):
            far(row, part, order[2], C_AT, order[:2])
            to_partner(row, part, order, 2)

    def finish(g):
        for row, part, order in each(g):
            for by in range(SIDE):
                ref = partner_ref(1 - c, part, order, by)
                remote(ref, row, PARTNER_AT + by, device(pos, 1 - c)).wait_recv()

    def halo(src, dst, slot, by):
        return pltpu.make_async_remote_copy(
            src_ref=src, dst_ref=dst, send_sem=halo_send.at[slot, by], recv_sem=halo_recv.at[slot, by],
            device_id=at_rank(by), device_id_type=MESH,
        )

    def norm(gain, r0, n):
        def step(k, carry):
            at = pl.ds(pl.multiple_of(r0 + k * 16, 16), 16)
            wide = res[at, :].astype(jnp.float32)
            power = jnp.mean(wide * wide, axis=-1, keepdims=True)
            nrm[at, :] = (wide * lax.rsqrt(power + EPS) * gain[...]).astype(jnp.bfloat16)
            return carry

        lax.fori_loop(0, n // 16, step, 0)

    def columns(at, n):
        return w[:, :, :, :, :, pl.ds(at, n)].reshape(width, n)

    def rotated(u):
        return u * cosine[...] + pltpu.roll(u, head // 2, 1) * sine[...]

    for copy in local:
        copy.wait()
    for g in range(4):
        first(g)
    for by in range(1, SPAN + 1):
        copy = halo(doc_row, marks.at[SPAN - by], 2, by)
        copy.start()
        sends.append(copy)
    marks[SPAN] = doc_row[...]

    tok_copies[0].wait()
    norm(gain_attn, 0, chunk)
    second(0)
    tok_copies[1].wait()
    norm(gain_attn, chunk, chunk)
    second_relay(0)
    tok_copies[2].wait()
    norm(gain_attn, 2 * chunk, chunk)
    third(0)
    second(1)
    tok_copies[3].wait()
    norm(gain_attn, 3 * chunk, chunk)
    third_relay(0)
    second_relay(1)
    third_near(0)
    third(1)
    third_far(0)
    finish(0)

    pair = jnp.dot(nrm[...], columns(512, 256), preferred_element_type=jnp.float32)
    keys[SPAN] = jnp.transpose(rotated(pair[:, :head])).astype(jnp.bfloat16)
    vals[SPAN] = pair[:, head:].astype(jnp.bfloat16)
    third_relay(1)
    second(2)
    for p in range(2):
        raw = jnp.dot(nrm[...], columns(256 * p, 256), preferred_element_type=jnp.float32)
        if p == 0:
            for by in range(1, SPAN + 1):
                for slot, buf in ((0, keys), (1, vals)):
                    copy = halo(buf.at[SPAN], buf.at[SPAN - by], slot, by)
                    copy.start()
                    sends.append(copy)
            second(3)
        for k in range(2):
            qry[2 * p + k] = rotated(raw[:, k * head : (k + 1) * head]).astype(jnp.bfloat16)
        if p == 0:
            third_near(1)
            second_relay(2)
    third(2)
    third_far(1)
    second_relay(3)

    for by in range(1, SPAN + 1):
        halo(doc_row, marks.at[SPAN - by], 2, by).wait_recv()
        for slot, buf in ((0, keys), (1, vals)):
            halo(buf.at[SPAN], buf.at[SPAN - by], slot, by).wait_recv()

    tall = rows // 2
    scale = math.log2(math.e) / math.sqrt(head)

    def attend(part, h):
        spans = (
            [(j, 0, rows) for j in range(SPAN)] + [(SPAN, 0, tall)]
            if part == 0
            else [(0, tall, tall)]
            + [(j, 0, rows) for j in range(1, SPAN)]
            + [(SPAN, 0, tall), (SPAN, tall, tall)]
        )
        q = qry[h, part * tall : (part + 1) * tall, :]
        mine = doc_col[part * tall : (part + 1) * tall, :]
        scores = []
        for k, (j, at, n) in enumerate(spans):
            s = jnp.dot(q, keys[j, :, at : at + n], preferred_element_type=jnp.float32)
            same = marks[j, 0:1, at : at + n] == mine
            if k == len(spans) - 1:
                same = same & (
                    lax.broadcasted_iota(jnp.int32, (tall, n), 1)
                    <= lax.broadcasted_iota(jnp.int32, (tall, n), 0)
                )
            scores.append(jnp.where(same, s, NEGATIVE))
        peak = functools.reduce(
            jnp.maximum, [jnp.max(s, axis=1, keepdims=True) for s in scores]
        )
        total = jnp.zeros((tall, 1), jnp.float32)
        mixed = jnp.zeros((tall, head), jnp.float32)
        for (j, at, n), s in zip(spans, scores):
            e = jnp.exp2((s - peak) * scale)
            total = total + jnp.sum(e, axis=1, keepdims=True)
            mixed = mixed + jnp.dot(
                e.astype(jnp.bfloat16), vals[j, at : at + n, :], preferred_element_type=jnp.float32
            )
        att[part * tall : (part + 1) * tall, pl.ds(pl.multiple_of(h * head, head), head)] = (
            mixed / total
        ).astype(jnp.bfloat16)

    def attend_heads(part, lo, hi):
        def step(h, carry):
            attend(part, h)
            return carry

        lax.fori_loop(lo, hi, step, 0)

    attend_heads(0, 0, 2)
    finish(1)
    third_relay(2)
    third(3)
    attend_heads(0, 2, 4)
    third_near(2)
    attend_heads(1, 0, 2)
    attend_heads(1, 2, 4)

    def wide_step(lhs, at, n, after):
        per = 2 * 2 * SIDE * shard

        def step(k, carry):
            for zz in range(2):
                rhs = w[k, 2 * zz : 2 * zz + 2, :, :, :, at : at + n].reshape(per, n)
                got = lax.dot_general(
                    lhs[...], rhs, (((1,), (1,)), ((), ())), preferred_element_type=jnp.float32
                )
                here = pl.ds(pl.multiple_of((k * 2 + zz) * per, per), per)
                res[:, here] = (res[:, here].astype(jnp.float32) + got).astype(jnp.bfloat16)
            after(k)
            return carry

        lax.fori_loop(0, SIDE, step, 0)

    wide_step(att, OUT_AT, 512, lambda k: None)
    third_relay(3)
    norm(gain_mlp, 0, rows // 2)
    third_far(2)
    norm(gain_mlp, rows // 2, rows // 2)
    finish(2)

    def gated(lo, hi):
        def step(j, carry):
            at = pl.multiple_of(j * 256, 256)
            gate = jnp.dot(nrm[...], columns(GATE_AT + at, 256), preferred_element_type=jnp.float32)
            up = jnp.dot(nrm[...], columns(UP_AT + at, 256), preferred_element_type=jnp.float32)
            hid[:, pl.ds(at, 256)] = (gate / (1.0 + jnp.exp(-gate)) * up).astype(jnp.bfloat16)
            return carry

        lax.fori_loop(lo, hi, step, 0)

    gated(0, 2)
    third_near(3)
    gated(2, 4)
    third_far(3)
    finish(3)

    slab = width // SIDE

    def put(k):
        here = pl.ds(pl.multiple_of(k * slab, slab), slab)
        return pltpu.make_async_copy(res.at[:, here], out.at[:, here], out_sem.at[k])

    wide_step(hid, DOWN_AT, 1024, lambda k: put(k).start())
    for k in range(SIDE):
        put(k).wait()
    for copy in sends:
        copy.wait_send()


def per_device(
    tokens, doc_ids, attn_gain, mlp_gain, w_query, w_key_value, w_out, w_gate, w_up, w_down
):
    rows, width = tokens.shape
    head = w_key_value.shape[1] // 2
    heads = w_query.shape[1] // head
    shard = w_query.shape[0]
    rank = lax.axis_index(("dp", "fsdp"))
    freqs = THETA ** (-2.0 * jnp.arange(head // 2, dtype=jnp.float32) / head)
    position = rank * rows + jnp.arange(rows, dtype=jnp.int32)
    angle = position.astype(jnp.float32)[:, None] * freqs[None, :]
    cosine = jnp.cos(angle)
    sine = jnp.sin(angle)
    cosine = jnp.concatenate([cosine, cosine], axis=1)
    sine = jnp.concatenate([-sine, sine], axis=1)
    doc_row = jnp.broadcast_to(doc_ids[None, :], (8, rows))
    vmem = pl.BlockSpec(memory_space=pltpu.VMEM)
    anywhere = pl.BlockSpec(memory_space=pl.ANY)
    bf16 = jnp.bfloat16
    return pl.pallas_call(
        kernel,
        out_shape=jax.ShapeDtypeStruct((rows, width), bf16),
        in_specs=[anywhere] + [vmem] * 6 + [anywhere] * 6,
        out_specs=anywhere,
        scratch_shapes=[
            pltpu.VMEM((SIDE, SIDE, 2, SIDE, shard, WIDTH), bf16),
            pltpu.VMEM((rows, width), bf16),
            pltpu.VMEM((rows, width), bf16),
            pltpu.VMEM((heads, rows, head), bf16),
            pltpu.VMEM((SPAN + 1, head, rows), bf16),
            pltpu.VMEM((SPAN + 1, rows, head), bf16),
            pltpu.VMEM((SPAN + 1, 8, rows), jnp.int32),
            pltpu.VMEM((rows, heads * head), bf16),
            pltpu.VMEM((rows, w_gate.shape[1]), bf16),
            pltpu.SemaphoreType.DMA((12, SLOTS)),
            pltpu.SemaphoreType.DMA((12, SLOTS)),
            pltpu.SemaphoreType.DMA((3, SPAN + 1)),
            pltpu.SemaphoreType.DMA((3, SPAN + 1)),
            pltpu.SemaphoreType.DMA((6,)),
            pltpu.SemaphoreType.DMA((4,)),
            pltpu.SemaphoreType.DMA((SIDE,)),
        ],
        compiler_params=pltpu.CompilerParams(
            collective_id=0, has_side_effects=True, vmem_limit_bytes=67043328
        ),
    )(
        tokens,
        attn_gain[None, :],
        mlp_gain[None, :],
        cosine,
        sine,
        doc_row,
        doc_ids[:, None],
        w_query,
        w_key_value,
        w_out.T,
        w_gate,
        w_up,
        w_down.T,
    )


def solution(mesh):
    every = ("dp", "fsdp")
    in_specs = (
        P(every, None), P(every), P(), P(), P(every, None), P(every, None),
        P(None, every), P(every, None), P(every, None), P(None, every),
    )
    return jax.shard_map(
        per_device, mesh=mesh, in_specs=in_specs, out_specs=P(every, None), check_vma=False
    )
```

time: 307 us -> 132 us (0.43)
  waiting for transfers between devices: 174 us -> 0 us
  Pallas kernels: 0 us -> 122 us
  matrix products: 45.4 us -> 0 us
  starting transfers between devices: 29.8 us -> 0 us
  blocking collectives: 22.2 us -> 0 us
  between operations: 13.5 us -> 0.02 us
  other arithmetic: 14.4 us -> 1.99 us
    all_gather x4 -> x0, waiting for transfers between devices: 168 us -> none  [the longest x2 80.3 us: sent_together(): out = lax.all_gather(both, axis, axis=dim, tiled=True)]
    pallas_call x0 -> x1, Pallas kernels: none -> 122 us  [per_device(): pl.pallas_call(kernel, out_shape=jax.ShapeDtypeStruct((rows, width), bf16...]
    dot_general x10 -> x0, matrix products: 45.4 us -> none  [the longest x1 10.2 us: per_device(): jnp.dot(hidden, lax.all_gather(w_down, ('dp', 'fsdp'), axis=1, tiled=True...]
    ppermute x8 -> x0, starting transfers between devices: 29.7 us -> none  [shifted(): return lax.ppermute(array, axis, pairs)]
    all_gather x2 -> x0, blocking collectives: 22.2 us -> none  [sent_together(): out = lax.all_gather(both, axis, axis=dim, tiled=True)]
    reduce_sum x5 -> x0, other arithmetic: 6.52 us -> none  [the longest x2 3.97 us: rms_scale(): power = jnp.mean(wide * wide, axis=-1, keepdims=True)]
    ppermute x8 -> x0, waiting for transfers between devices: 5.47 us -> none  [shifted(): return lax.ppermute(array, axis, pairs)]
  transfers between devices with their start and end apart: 12 -> 0, of which waited for: 6 -> 0; matrix products, arithmetic and copies ran while one was open for 16% -> 0% of each run, Pallas kernels for 0% -> 0%
where the time goes in v1:
time: 132 us
  Pallas kernels  122 us (92%)
  local copies, waits for them, and re-layouts  7.52 us (6%)
  other arithmetic  1.99 us (2%)
    pallas_call x1, Pallas kernels, per_device(): pl.pallas_call(kernel, out_shape=jax.ShapeDtypeStruct((rows, width), bf16...  122 us
    unnamed x1, local copies, waits for them, and re-layouts  4.7 us

profile of v1, /device:TPU:1, one launch (start us, length us, event | category | flops | bytes accessed | tf_op | source)
XLA Modules:
  0.0 131.7 jit_solution(10839094166875100211)
XLA Ops:
  0.0 1.3 broadcast_in_dim.19.doc_row
  1.3 1.5 %copy.11.doc_col = s32[512,1]{1,0:T(8,128)} copy(s32[512,1]{0,1:T(1,128)} %bitcast.9) | data formatting | bytes 4096 | tf_op jit(solution)/shard_map/broadcast_in_dim | solution.py:431
  2.8 1.0 fusion
  3.8 1.0 pad_maximum_fusion
  4.8 122.2 %shard_map.100 = bf16[512,4096]{1,0:T(8,128)(2,1)} custom-call(bf16[512,4096]{1,0:T(8,128)(2,1)} %tok.1, f32[1,4096]{1,0:T(1,128)} %bitcast.7, f32[1,4096]{1,0:T(1,128)} %bitcast.8, f32[512,128]{1,0:T(8,128)} %get-tuple-element.8.cosine, f32[512,128]{1,0:T(8,128)} %get-tuple-element.9.sine, s32[8,512]{1,0:T(8,128)} %broadcast_in_dim.19.doc_row, ...), custom_call_target="tpu_custom_call" | custom-call | tf_op jit(solution)/shard_map/pallas_call | solution.py:398
  127.0 4.7 %copy.13 = bf16[512,4096]{1,0:T(8,128)(2,1)} copy(bf16[512,4096]{1,0:T(8,128)(2,1)} %shard_map.100) | data formatting | bytes 8388608
  (2 shorter events, 0.0 us)

commit v2 on v1

v2 whole, which is shorter than its diff:
```python
import functools
import math

import jax
import jax.numpy as jnp
import numpy as np
from jax import lax
from jax.experimental import pallas as pl
from jax.experimental.pallas import tpu as pltpu
from jax.sharding import PartitionSpec as P

MESH = pl.DeviceIdType.MESH
EPS = 1e-05
THETA = 500000.0
NEGATIVE = -1e30
SIDE = 4
SPAN = 4
GROUPS = (
    ((0, 128, 0), (128, 128, 2)),
    ((256, 384, 0), (640, 256, 1), (896, 512, 2)),
    ((1408, 640, 0), (2048, 640, 1), (2688, 640, 2)),
    ((3328, 256, 0), (3584, 384, 1), (3968, 384, 2)),
)
ORDERS = (("x", "y", "z"), ("y", "z", "x"), ("z", "x", "y"))
PAIR_AT, QUERY_AT, OUT_AT, GATE_AT, UP_AT, DOWN_AT, WIDTH = 0, 256, 768, 1280, 2304, 3328, 4352
ARRIVALS = 104


def kernel(
    tok, gain_attn, gain_mlp, freqs, docs, wq, wkv, wo, wg, wu, wd,
    res,
    w, nrm, qry, keys, vals, marks, mine, cosine, sine, power, att, hid,
    send, recv, local_sem, tok_sem,
):
    rows, width = res.shape
    head = qry.shape[2]
    shard = wq.shape[0]
    half = shard // 2
    dp = lax.axis_index("dp")
    x = lax.axis_index("fsdp")
    y = dp // (2 * SIDE)
    z = (dp // 2) % SIDE
    c = dp % 2
    pos = {"x": x, "y": y, "z": z}
    rank = dp * SIDE + x
    ranks = 32 * SIDE

    def device(at, core):
        return ((at["y"] * SIDE + at["z"]) * 2 + core, at["x"])

    def shift(dim, by):
        return {**pos, dim: (pos[dim] + by) % SIDE}

    def peer(dim, by):
        return device(shift(dim, by), c)

    def at_rank(by):
        other = (rank + by + ranks) % ranks
        return (other // SIDE, other % SIDE)

    local = []
    for k, (src, at) in enumerate(
        ((wkv, PAIR_AT), (wq, QUERY_AT), (wo, OUT_AT), (wg, GATE_AT), (wu, UP_AT), (wd, DOWN_AT))
    ):
        local.append(
            pltpu.make_async_copy(
                src, w.at[y, z, c, x, :, pl.ds(at, src.shape[1])], local_sem.at[0]
            )
        )
    for copy in local:
        copy.start()
    chunk = rows // 4
    tok_copies = [
        pltpu.make_async_copy(
            tok.at[pl.ds(k * chunk, chunk)], res.at[pl.ds(k * chunk, chunk)], tok_sem.at[k]
        )
        for k in range(4)
    ]
    for copy in tok_copies:
        copy.start()

    barrier = pltpu.get_barrier_semaphore()
    friends = [peer(dim, by) for dim in ("x", "y", "z") for by in (1, 2, 3)]
    friends.append(device(pos, 1 - c))
    friends += [at_rank(by) for by in range(-SPAN, SPAN + 1) if by != 0]
    for friend in friends:
        pl.semaphore_signal(barrier, inc=1, device_id=friend, device_id_type=MESH)
    pl.semaphore_wait(barrier, len(friends))

    arrivals = {}

    def arrival(*key):
        return recv.at[arrivals.setdefault(key, len(arrivals))]

    def block(core, sel, part, r0, nr):
        at, n = part
        return w.at[
            sel["y"], sel["z"], core, sel["x"], pl.ds(r0, nr), pl.ds(at, n)
        ]

    def remote(ref, key, to, sent=0):
        return pltpu.make_async_remote_copy(
            src_ref=ref, dst_ref=ref, send_sem=send.at[sent], recv_sem=arrival(*key),
            device_id=to, device_id_type=MESH,
        )

    def push(ref, key, to, sent):
        remote(ref, key, to, sent).start()

    ALL = slice(None)

    def each(g):
        for p, (at, n, o) in enumerate(GROUPS[g]):
            yield g * 3 + p, (at, n), ORDERS[o]

    def keys_of(row, k):
        at = (row, k)
        near_key, far_key = ((*at, 2), (*at, 2)) if k < 2 else ((*at, 2), (*at, 3))
        return (*at, 0), (*at, 1), near_key, far_key

    def spread(row, part, order, k):
        dim = order[k]
        up, down, close, _ = keys_of(row, k)
        sel = {**pos, **{d: ALL for d in order[:k]}}
        push(block(c, sel, part, 0, half), up, peer(dim, 1), k)
        push(block(c, sel, part, half, half), down, peer(dim, -1), k)
        push(block(c, sel, part, half, half), close, peer(dim, 1), k)
        push(block(c, sel, part, 0, half), close, peer(dim, -1), k)

    def relay(row, part, order, k):
        dim = order[k]
        up, down, _, distant = keys_of(row, k)
        back = {**shift(dim, -1), **{d: ALL for d in order[:k]}}
        ahead = {**shift(dim, 1), **{d: ALL for d in order[:k]}}
        ref = block(c, back, part, 0, half)
        remote(ref, up, peer(dim, 1)).wait_recv()
        push(ref, distant, peer(dim, 1), k)
        ref = block(c, ahead, part, half, half)
        remote(ref, down, peer(dim, 1)).wait_recv()
        push(ref, distant, peer(dim, -1), k)

    def whole(row, part, order, k, blocks, key):
        dim = order[k]
        sel = {**pos, dim: pl.ds(0, blocks), **{d: ALL for d in order[:k]}}
        remote(block(c, sel, part, 0, shard), key, peer(dim, 1)).wait_recv()

    def near(row, part, order, k):
        whole(row, part, order, k, 1, keys_of(row, k)[2])

    def far(row, part, order, k):
        whole(row, part, order, k, 1, keys_of(row, k)[3])

    def both(row, part, order, k):
        whole(row, part, order, k, 2, keys_of(row, k)[2])

    def ring(k, what, g, only=None):
        for row, part, order in each(g):
            if only is None or order[2] in only:
                what(row, part, order, k)

    def direct(k, g):
        for row, part, order in each(g):
            sel = {**pos, **{d: ALL for d in order[:k]}}
            for by in (1, 3, 2):
                push(block(c, sel, part, 0, shard), ("direct", k, g), peer(order[k], by), k)

    def span(g):
        lo, hi = GROUPS[g][0], GROUPS[g][-1]
        return pl.ds(lo[0], hi[0] + hi[1] - lo[0])

    def direct_wait(k, g):
        three = pl.ds(0, 3)
        ref = w.at[0, three, 0, ALL, ALL, span(g)] if k else w.at[0, 0, 0, three, ALL, span(g)]
        remote(ref, ("direct", k, g), device(pos, 1 - c)).wait_recv()

    def partner_ref(core, part, order, by):
        sel = {order[0]: ALL, order[1]: ALL, order[2]: (pos[order[2]] + by) % SIDE}
        return block(core, sel, part, 0, shard)

    def share(g, *which):
        for row, part, order in each(g):
            for by in which:
                push(partner_ref(c, part, order, by), ("share", g), device(pos, 1 - c), 3)

    def share_wait(g):
        ref = w.at[ALL, ALL, 1 - c, ALL, ALL, span(g)]
        remote(ref, ("share", g), device(pos, 1 - c)).wait_recv()

    def halo(src, dst, slot, by, to):
        key = ("halo", slot, by) if (slot, by) in ((0, 1), (1, 3)) else ("halo", slot)
        return pltpu.make_async_remote_copy(
            src_ref=src, dst_ref=dst, send_sem=send.at[4 + slot], recv_sem=arrival(*key),
            device_id=at_rank(to), device_id_type=MESH,
        )

    def norm(gain, r0, n):
        def step(k, carry):
            at = pl.ds(pl.multiple_of(r0 + k * 16, 16), 16)
            wide = res[at, :].astype(jnp.float32)
            power = jnp.mean(wide * wide, axis=-1, keepdims=True)
            nrm[at, :] = (wide * lax.rsqrt(power + EPS) * gain[...]).astype(jnp.bfloat16)
            return carry

        lax.fori_loop(0, n // 16, step, 0)

    def columns(at, n):
        return w[:, :, :, :, :, pl.ds(at, n)].reshape(width, n)

    def rotated(u):
        return u * cosine[...] + pltpu.roll(u, head // 2, 1) * sine[...]

    scope = jax.named_scope

    def pass_on(src, dst, slot, by, to):
        halo(src, dst, slot, by, to).start()

    def halo_wait(slot, by):
        buf = (keys, vals)[slot]
        halo(buf.at[SPAN], buf.at[SPAN - by], slot, by, by).wait_recv()

    def halo_rest(slot, n):
        ref = (keys, vals, marks)[slot].at[pl.ds(0, n)]
        halo(ref, ref, slot, 4, 4).wait_recv()

    marks[SPAN] = jnp.broadcast_to(docs[...], (8, rows))
    with scope("local"):
        own = w.at[y, z, c, x]
        pltpu.make_async_copy(own, own, local_sem.at[0]).wait()
    for g in (0, 1):
        direct(0, g)
    for g in (2, 3):
        ring(0, spread, g)
    turned = docs[...].astype(jnp.float32)
    mine[...] = jnp.transpose(jnp.broadcast_to(turned, (head, rows))).astype(jnp.int32)
    with scope("norm0"):
        tok_copies[0].wait()
        norm(gain_attn, 0, chunk)
    with scope("B0"):
        direct_wait(0, 0)
        direct(1, 0)
    with scope("B1"):
        direct_wait(0, 1)
        ring(1, spread, 1)
    with scope("Ar"):
        for g in (2, 3):
            ring(0, relay, g)
    for by in range(1, SPAN + 1):
        pass_on(marks.at[SPAN], marks.at[SPAN - by], 2, by, by)
    with scope("norm1"):
        tok_copies[1].wait()
        norm(gain_attn, chunk, chunk)
    with scope("C0"):
        direct_wait(1, 0)
        ring(2, spread, 0)
        share(0, 0)
    with scope("B2"):
        ring(0, both, 2)
        ring(1, spread, 2)
    with scope("norm2"):
        tok_copies[2].wait()
        norm(gain_attn, 2 * chunk, chunk)
    with scope("Br1"):
        ring(1, relay, 1)
    with scope("B3"):
        ring(0, both, 3)
        ring(1, spread, 3)
    with scope("Cr0"):
        ring(2, relay, 0)
    with scope("angles"):
        place = rank * rows + lax.broadcasted_iota(jnp.int32, (rows, head), 0)
        angle = place.astype(jnp.float32) * freqs[...]
        cosine[...] = jnp.cos(angle)
        turn = jnp.sin(angle)
        early = lax.broadcasted_iota(jnp.int32, (rows, head), 1) < head // 2
        sine[...] = jnp.where(early, -turn, turn)
    with scope("near0"):
        ring(2, near, 0)
        share(0, 1, 3)
    with scope("Br2"):
        ring(1, relay, 2)
    with scope("C1"):
        ring(1, both, 1)
        ring(2, spread, 1)
    with scope("norm3"):
        tok_copies[3].wait()
        norm(gain_attn, 3 * chunk, chunk)
    with scope("far0"):
        ring(2, far, 0)
        share(0, 2)
    with scope("Br3"):
        ring(1, relay, 3)
    with scope("F0"):
        share_wait(0)

    with scope("pair"):
        pair = jnp.dot(nrm[...], columns(PAIR_AT, 256), preferred_element_type=jnp.float32)
        keys[SPAN] = jnp.transpose(rotated(pair[:, :head])).astype(jnp.bfloat16)
        vals[SPAN] = pair[:, head:].astype(jnp.bfloat16)
    pass_on(keys.at[SPAN], keys.at[SPAN - 1], 0, 1, 1)
    pass_on(vals.at[SPAN], vals.at[SPAN - 3], 1, 3, 3)
    pass_on(vals.at[SPAN], vals.at[SPAN - 1], 1, 1, 1)
    pass_on(keys.at[SPAN], keys.at[SPAN - 3], 0, 3, 3)
    pass_on(keys.at[SPAN], keys.at[SPAN - 4], 0, 4, 4)
    pass_on(vals.at[SPAN], vals.at[SPAN - 4], 1, 4, 4)
    with scope("Cr1zx"):
        share(1, 0)
        ring(2, relay, 1, "zx")
    with scope("Cr1y"):
        ring(2, relay, 1, "y")
    with scope("C2yz"):
        ring(1, both, 2)
        ring(2, spread, 2, "yz")
    with scope("forward"):
        halo_wait(0, 1)
        pass_on(keys.at[SPAN - 1], keys.at[SPAN - 2], 0, 2, 1)
        halo_wait(1, 3)
        pass_on(vals.at[SPAN - 3], vals.at[SPAN - 2], 1, 2, -1)
    with scope("C2x"):
        ring(2, spread, 2, "x")
    with scope("near1"):
        ring(2, near, 1)
        share(1, 1, 3)
    with scope("far1"):
        ring(2, far, 1)
        share(1, 2)
    with scope("F1"):
        share_wait(1)
        share(2, 0)
    with scope("query"):
        for p in range(2):
            raw = jnp.dot(nrm[...], columns(QUERY_AT + 256 * p, 256), preferred_element_type=jnp.float32)
            for k in range(2):
                qry[2 * p + k] = rotated(raw[:, k * head : (k + 1) * head]).astype(jnp.bfloat16)
    with scope("halo"):
        halo_rest(2, 4)
        halo_rest(0, 3)
        halo_rest(1, 3)

    tall = rows // 2
    scale = math.log2(math.e) / math.sqrt(head)

    def attend(part, h):
        spans = (
            [(j, 0, rows) for j in range(SPAN)] + [(SPAN, 0, tall)]
            if part == 0
            else [(0, tall, tall)]
            + [(j, 0, rows) for j in range(1, SPAN)]
            + [(SPAN, 0, tall), (SPAN, tall, tall)]
        )
        q = qry[h, part * tall : (part + 1) * tall, :]
        own = mine[part * tall : (part + 1) * tall, 0:1]
        scores = []
        for k, (j, at, n) in enumerate(spans):
            s = jnp.dot(q, keys[j, :, at : at + n], preferred_element_type=jnp.float32)
            same = marks[j, 0:1, at : at + n] == own
            if k == len(spans) - 1:
                same = same & (
                    lax.broadcasted_iota(jnp.int32, (tall, n), 1)
                    <= lax.broadcasted_iota(jnp.int32, (tall, n), 0)
                )
            scores.append(jnp.where(same, s, NEGATIVE))
        peak = functools.reduce(
            jnp.maximum, [jnp.max(s, axis=1, keepdims=True) for s in scores]
        )
        total = jnp.zeros((tall, 1), jnp.float32)
        mixed = jnp.zeros((tall, head), jnp.float32)
        for (j, at, n), s in zip(spans, scores):
            e = jnp.exp2((s - peak) * scale)
            total = total + jnp.sum(e, axis=1, keepdims=True)
            mixed = mixed + jnp.dot(
                e.astype(jnp.bfloat16), vals[j, at : at + n, :], preferred_element_type=jnp.float32
            )
        att[part * tall : (part + 1) * tall, pl.ds(pl.multiple_of(h * head, head), head)] = (
            mixed / total
        ).astype(jnp.bfloat16)

    def attend_heads(part, lo, hi):
        def step(h, carry):
            attend(part, h)
            return carry

        lax.fori_loop(lo, hi, step, 0)

    with scope("attend0"):
        attend_heads(0, 0, 2)
    with scope("Cr2"):
        ring(2, relay, 2)
    with scope("C3"):
        ring(1, both, 3)
        ring(2, spread, 3)
    with scope("attend1"):
        attend_heads(0, 2, 4)
    with scope("attend2"):
        attend_heads(1, 0, 2)
    with scope("near2"):
        ring(2, near, 2)
        share(2, 1, 3)
        share(3, 0)
    with scope("attend3"):
        attend_heads(1, 2, 4)

    def wide_step(lhs, at, n, after, squares=False):
        per = 2 * 2 * SIDE * shard

        def step(k, carry):
            for zz in range(2):
                rhs = w[k, 2 * zz : 2 * zz + 2, :, :, :, at : at + n].reshape(per, n)
                got = lax.dot_general(
                    lhs[...], rhs, (((1,), (1,)), ((), ())), preferred_element_type=jnp.float32
                )
                here = pl.ds(pl.multiple_of((k * 2 + zz) * per, per), per)
                new = (res[:, here].astype(jnp.float32) + got).astype(jnp.bfloat16)
                res[:, here] = new
                if squares:
                    wide = new.astype(jnp.float32)
                    wide = wide * wide
                    sums = [wide[:, i * head : (i + 1) * head] for i in range(per // head)]
                    power[...] += functools.reduce(jnp.add, sums)
            after(k)
            return carry

        lax.fori_loop(0, SIDE, step, 0)

    def scaled(gain):
        mean = jnp.sum(power[...], axis=-1, keepdims=True) / width
        power[...] = jnp.broadcast_to(lax.rsqrt(mean + EPS), (rows, head))

        def step(k, carry):
            at = pl.ds(pl.multiple_of(k * 32, 32), 32)
            inverse = power[at, :]
            for i in range(width // head):
                lanes = slice(i * head, (i + 1) * head)
                wide = res[at, lanes].astype(jnp.float32)
                nrm[at, lanes] = (wide * inverse * gain[:, lanes]).astype(jnp.bfloat16)
            return carry

        lax.fori_loop(0, rows // 32, step, 0)

    power[...] = jnp.zeros_like(power)
    with scope("project"):
        wide_step(att, OUT_AT, 512, lambda k: None, squares=True)
    with scope("far2"):
        ring(2, far, 2)
        share(2, 2)
    with scope("mlp_norm"):
        scaled(gain_mlp)
    with scope("Cr3"):
        ring(2, relay, 3)
    with scope("F2"):
        share_wait(2)

    def gated(lo, hi):
        def step(j, carry):
            at = pl.multiple_of(j * 256, 256)
            gate = jnp.dot(nrm[...], columns(GATE_AT + at, 256), preferred_element_type=jnp.float32)
            up = jnp.dot(nrm[...], columns(UP_AT + at, 256), preferred_element_type=jnp.float32)
            hid[:, pl.ds(at, 256)] = (gate / (1.0 + jnp.exp(-gate)) * up).astype(jnp.bfloat16)
            return carry

        lax.fori_loop(lo, hi, step, 0)

    with scope("gated0"):
        gated(0, 2)
    with scope("near3"):
        ring(2, near, 3)
        share(3, 1, 3)
    with scope("gated1"):
        gated(2, 4)
    with scope("F3"):
        ring(2, far, 3)
        share(3, 2)
        share_wait(3)

    with scope("down"):
        wide_step(hid, DOWN_AT, 1024, lambda k: None)
    assert len(arrivals) <= ARRIVALS
    with scope("sent"):
        three = pl.ds(0, 3)
        for k, ref in enumerate(
            (w.at[0, 0, 0, three], w.at[0, three, 0], w.at[three, ALL, 0], w.at[ALL, ALL, 0])
        ):
            remote(ref, ("share", 0), device(pos, 1 - c), k).wait_send()
        for slot, buf in enumerate((keys, vals, marks)):
            ref = buf.at[pl.ds(0, 4)]
            halo(ref, ref, slot, 4, 4).wait_send()


def per_device(
    tokens, doc_ids, attn_gain, mlp_gain, w_query, w_key_value, w_out, w_gate, w_up, w_down
):
    rows, width = tokens.shape
    head = w_key_value.shape[1] // 2
    heads = w_query.shape[1] // head
    shard = w_query.shape[0]
    freqs = THETA ** (-2.0 * np.arange(head // 2) / head)
    freqs = np.concatenate([freqs, freqs])[None, :].astype(np.float32)
    vmem = pl.BlockSpec(memory_space=pltpu.VMEM)
    anywhere = pl.BlockSpec(memory_space=pl.ANY)
    bf16 = jnp.bfloat16
    return pl.pallas_call(
        kernel,
        out_shape=pltpu.VMEM((rows, width), bf16),
        in_specs=[anywhere] + [vmem] * 4 + [anywhere] * 6,
        out_specs=vmem,
        scratch_shapes=[
            pltpu.VMEM((SIDE, SIDE, 2, SIDE, shard, WIDTH), bf16),
            pltpu.VMEM((rows, width), bf16),
            pltpu.VMEM((heads, rows, head), bf16),
            pltpu.VMEM((SPAN + 1, head, rows), bf16),
            pltpu.VMEM((SPAN + 1, rows, head), bf16),
            pltpu.VMEM((SPAN + 1, 8, rows), jnp.int32),
            pltpu.VMEM((rows, head), jnp.int32),
            pltpu.VMEM((rows, head), jnp.float32),
            pltpu.VMEM((rows, head), jnp.float32),
            pltpu.VMEM((rows, head), jnp.float32),
            pltpu.VMEM((rows, heads * head), bf16),
            pltpu.VMEM((rows, w_gate.shape[1]), bf16),
            pltpu.SemaphoreType.DMA((7,)),
            pltpu.SemaphoreType.DMA((ARRIVALS,)),
            pltpu.SemaphoreType.DMA((1,)),
            pltpu.SemaphoreType.DMA((4,)),
        ],
        compiler_params=pltpu.CompilerParams(
            collective_id=0, has_side_effects=True, vmem_limit_bytes=58 * 1024 * 1024
        ),
    )(
        tokens,
        attn_gain[None, :],
        mlp_gain[None, :],
        jnp.asarray(freqs),
        doc_ids[None, :],
        w_query,
        w_key_value,
        w_out.T,
        w_gate,
        w_up,
        w_down.T,
    )


def solution(mesh):
    every = ("dp", "fsdp")
    in_specs = (
        P(every, None), P(every), P(), P(), P(every, None), P(every, None),
        P(None, every), P(every, None), P(every, None), P(None, every),
    )
    return jax.shard_map(
        per_device, mesh=mesh, in_specs=in_specs, out_specs=P(every, None), check_vma=False
    )
```

time: 132 us -> 101 us (0.77)
  Pallas kernels: 122 us -> 98.3 us
  local copies, waits for them, and re-layouts: 7.52 us -> 2.02 us
  other arithmetic: 1.99 us -> 0 us
    pallas_call x1, Pallas kernels: 122 us -> 98.3 us  [per_device(): pl.pallas_call(kernel, out_shape=pltpu.VMEM((rows, width), bf16), in_spec...]
    broadcast_in_dim x2 -> x0, local copies, waits for them, and re-layouts: 2.82 us -> none  [the longest x1 1.54 us: per_device(): doc_ids[:, None]]
    unnamed x1, local copies, waits for them, and re-layouts: 4.7 us -> 2.02 us
where the time goes in v2:
time: 101 us; the launch traced here: 100 us
  Pallas kernels  98.3 us (97%)
  local copies, waits for them, and re-layouts  2.02 us (2%)
    pallas_call x1, Pallas kernels, per_device(): pl.pallas_call(kernel, out_shape=pltpu.VMEM((rows, width), bf16), in_spec...  98.3 us

profile of v2, /device:TPU:1, one launch (start us, length us, event | category | flops | bytes accessed | tf_op | source)
XLA Modules:
  0.0 100.3 jit_solution(5443888861703191585)
XLA Ops:
  0.0 98.3 %shard_map.109 = bf16[512,4096]{1,0:T(8,128)(2,1)S(1)} custom-call(bf16[512,4096]{1,0:T(8,128)(2,1)} %tok.1, f32[1,4096]{1,0:T(1,128)} %bitcast.7, f32[1,4096]{1,0:T(1,128)} %bitcast.8, f32[1,128]{1,0:T(1,128)} %constant.2.clone.freqs, s32[1,512]{1,0:T(1,128)} %bitcast.9, bf16[32,512]{1,0:T(8,128)(2,1)} %wq.1, bf16[32,256]{1,0:T(8,128)(2,1)} %wkv.1, ...), custom_call_target="tpu_custom_call" | custom-call | tf_op jit(solution)/shard_map/pallas_call | solution.py:500
  98.3 2.0 %copy.13 = bf16[512,4096]{1,0:T(8,128)(2,1)} copy(bf16[512,4096]{1,0:T(8,128)(2,1)S(1)} %shard_map.109) | data formatting | bytes 8388608

commit v3 on v2

--- a/solution.py
+++ b/solution.py
@@ -16,24 +16,27 @@
 SIDE = 4
 SPAN = 4
 GROUPS = (
-    ((0, 128, 0), (128, 128, 2)),
-    ((256, 384, 0), (640, 256, 1), (896, 512, 2)),
-    ((1408, 640, 0), (2048, 640, 1), (2688, 640, 2)),
-    ((3328, 256, 0), (3584, 384, 1), (3968, 384, 2)),
+    ((0, 256, 0), (256, 256, 1), (512, 256, 2)),
+    ((768, 256, 0), (1024, 256, 1), (1280, 256, 2)),
+    ((1536, 256, 0), (1792, 256, 1), (2048, 256, 2)),
+    ((2304, 384, 0), (2688, 256, 1), (2944, 384, 2)),
+    ((3328, 128, 0), (3456, 128, 1), (3584, 256, 2)),
+    ((3840, 128, 0), (3968, 256, 1), (4224, 128, 2)),
 )
 ORDERS = (("x", "y", "z"), ("y", "z", "x"), ("z", "x", "y"))
-PAIR_AT, QUERY_AT, OUT_AT, GATE_AT, UP_AT, DOWN_AT, WIDTH = 0, 256, 768, 1280, 2304, 3328, 4352
-ARRIVALS = 104
+PAIR_AT, QUERY_AT, OUT_AT, DOWN_AT, LAST, WIDTH = 0, 256, 768, 3328, 512, 4352
+GATE_AT, UP_AT = (1280, 2304), (1792, 2816)
+ARRIVALS = 180
 
 
 def kernel(
     tok, gain_attn, gain_mlp, freqs, docs, wq, wkv, wo, wg, wu, wd,
     res,
-    w, nrm, qry, keys, vals, marks, mine, cosine, sine, power, att, hid,
+    w, nrm, qry, keys, vals, marks, mine, cosine, sine, power, peaks, sums, mixes, att, hid, acc,
     send, recv, local_sem, tok_sem,
 ):
     rows, width = res.shape
-    head = qry.shape[2]
+    heads, _, head = qry.shape
     shard = wq.shape[0]
     half = shard // 2
     dp = lax.axis_index("dp")
@@ -59,8 +62,11 @@
         return (other // SIDE, other % SIDE)
 
     local = []
-    for k, (src, at) in enumerate(
-        ((wkv, PAIR_AT), (wq, QUERY_AT), (wo, OUT_AT), (wg, GATE_AT), (wu, UP_AT), (wd, DOWN_AT))
+    some = wg.shape[1] // 2
+    for src, at in (
+        (wkv, PAIR_AT), (wq, QUERY_AT), (wo, OUT_AT), (wd, DOWN_AT),
+        (wg.at[:, pl.ds(0, some)], GATE_AT[0]), (wg.at[:, pl.ds(some, some)], GATE_AT[1]),
+        (wu.at[:, pl.ds(0, some)], UP_AT[0]), (wu.at[:, pl.ds(some, some)], UP_AT[1]),
     ):
         local.append(
             pltpu.make_async_copy(
@@ -110,7 +116,8 @@
     ALL = slice(None)
 
     def each(g):
-        for p, (at, n, o) in enumerate(GROUPS[g]):
+        for p in (2, 0, 1) if g else (0, 2, 1):
+            at, n, o = GROUPS[g][p]
             yield g * 3 + p, (at, n), ORDERS[o]
 
     def keys_of(row, k):
@@ -127,17 +134,24 @@
         push(block(c, sel, part, half, half), close, peer(dim, 1), k)
         push(block(c, sel, part, 0, half), close, peer(dim, -1), k)
 
+    def downwards(row, order, k):
+        return k == 2 and row // 3 in (1, 2) and order[2] != "x"
+
     def relay(row, part, order, k):
         dim = order[k]
-        up, down, _, distant = keys_of(row, k)
+        up, down, close, distant = keys_of(row, k)
         back = {**shift(dim, -1), **{d: ALL for d in order[:k]}}
         ahead = {**shift(dim, 1), **{d: ALL for d in order[:k]}}
         ref = block(c, back, part, 0, half)
         remote(ref, up, peer(dim, 1)).wait_recv()
-        push(ref, distant, peer(dim, 1), k)
+        if not downwards(row, order, k):
+            push(ref, distant, peer(dim, 1), k)
         ref = block(c, ahead, part, half, half)
         remote(ref, down, peer(dim, 1)).wait_recv()
         push(ref, distant, peer(dim, -1), k)
+        if downwards(row, order, k):
+            whole(row, part, order, k, 1, close)
+            push(block(c, ahead, part, 0, half), distant, peer(dim, -1), k)
 
     def whole(row, part, order, k, blocks, key):
         dim = order[k]
@@ -145,7 +159,8 @@
         remote(block(c, sel, part, 0, shard), key, peer(dim, 1)).wait_recv()
 
     def near(row, part, order, k):
-        whole(row, part, order, k, 1, keys_of(row, k)[2])
+        if not downwards(row, order, k):
+            whole(row, part, order, k, 1, keys_of(row, k)[2])
 
     def far(row, part, order, k):
         whole(row, part, order, k, 1, keys_of(row, k)[3])
@@ -177,17 +192,21 @@
         sel = {order[0]: ALL, order[1]: ALL, order[2]: (pos[order[2]] + by) % SIDE}
         return block(core, sel, part, 0, shard)
 
+    def shared(row, g):
+        return ("share", g, row if g == 0 else 0)
+
     def share(g, *which):
         for row, part, order in each(g):
             for by in which:
-                push(partner_ref(c, part, order, by), ("share", g), device(pos, 1 - c), 3)
-
-    def share_wait(g):
-        ref = w.at[ALL, ALL, 1 - c, ALL, ALL, span(g)]
-        remote(ref, ("share", g), device(pos, 1 - c)).wait_recv()
+                push(partner_ref(c, part, order, by), shared(row, g), device(pos, 1 - c), 3)
+
+    def share_wait(g, row=0):
+        cols = pl.ds(*GROUPS[0][row][:2]) if g == 0 else span(g)
+        ref = w.at[ALL, ALL, 1 - c, ALL, ALL, cols]
+        remote(ref, shared(row, g), device(pos, 1 - c)).wait_recv()
 
     def halo(src, dst, slot, by, to):
-        key = ("halo", slot, by) if (slot, by) in ((0, 1), (1, 3)) else ("halo", slot)
+        key = ("halo", slot, by) if (slot, by) in ((0, 1), (1, 3), (1, 1)) else ("halo", slot)
         return pltpu.make_async_remote_copy(
             src_ref=src, dst_ref=dst, send_sem=send.at[4 + slot], recv_sem=arrival(*key),
             device_id=at_rank(to), device_id_type=MESH,
@@ -226,9 +245,8 @@
     with scope("local"):
         own = w.at[y, z, c, x]
         pltpu.make_async_copy(own, own, local_sem.at[0]).wait()
-    for g in (0, 1):
-        direct(0, g)
-    for g in (2, 3):
+    direct(0, 0)
+    for g in range(1, 6):
         ring(0, spread, g)
     turned = docs[...].astype(jnp.float32)
     mine[...] = jnp.transpose(jnp.broadcast_to(turned, (head, rows))).astype(jnp.int32)
@@ -238,17 +256,17 @@
     with scope("B0"):
         direct_wait(0, 0)
         direct(1, 0)
-    with scope("B1"):
-        direct_wait(0, 1)
-        ring(1, spread, 1)
     with scope("Ar"):
-        for g in (2, 3):
+        for g in range(1, 6):
             ring(0, relay, g)
     for by in range(1, SPAN + 1):
         pass_on(marks.at[SPAN], marks.at[SPAN - by], 2, by, by)
     with scope("norm1"):
         tok_copies[1].wait()
         norm(gain_attn, chunk, chunk)
+    with scope("B1"):
+        ring(0, both, 1)
+        ring(1, spread, 1)
     with scope("C0"):
         direct_wait(1, 0)
         ring(2, spread, 0)
@@ -261,11 +279,6 @@
         norm(gain_attn, 2 * chunk, chunk)
     with scope("Br1"):
         ring(1, relay, 1)
-    with scope("B3"):
-        ring(0, both, 3)
-        ring(1, spread, 3)
-    with scope("Cr0"):
-        ring(2, relay, 0)
     with scope("angles"):
         place = rank * rows + lax.broadcasted_iota(jnp.int32, (rows, head), 0)
         angle = place.astype(jnp.float32) * freqs[...]
@@ -273,6 +286,15 @@
         turn = jnp.sin(angle)
         early = lax.broadcasted_iota(jnp.int32, (rows, head), 1) < head // 2
         sine[...] = jnp.where(early, -turn, turn)
+    with scope("Cr0"):
+        ring(2, relay, 0)
+    with scope("B345"):
+        for g in (3, 4, 5):
+            ring(0, both, g)
+            ring(1, spread, g)
+    with scope("norm3"):
+        tok_copies[3].wait()
+        norm(gain_attn, 3 * chunk, chunk)
     with scope("near0"):
         ring(2, near, 0)
         share(0, 1, 3)
@@ -281,79 +303,65 @@
     with scope("C1"):
         ring(1, both, 1)
         ring(2, spread, 1)
-    with scope("norm3"):
-        tok_copies[3].wait()
-        norm(gain_attn, 3 * chunk, chunk)
     with scope("far0"):
-        ring(2, far, 0)
-        share(0, 2)
-    with scope("Br3"):
-        ring(1, relay, 3)
+        for row, part, order in each(0):
+            far(row, part, order, 2)
+            push(partner_ref(c, part, order, 2), shared(row, 0), device(pos, 1 - c), 3)
     with scope("F0"):
-        share_wait(0)
+        share_wait(0, 0)
 
     with scope("pair"):
         pair = jnp.dot(nrm[...], columns(PAIR_AT, 256), preferred_element_type=jnp.float32)
         keys[SPAN] = jnp.transpose(rotated(pair[:, :head])).astype(jnp.bfloat16)
         vals[SPAN] = pair[:, head:].astype(jnp.bfloat16)
+    with scope("Br345"):
+        for g in (3, 4, 5):
+            ring(1, relay, g)
     pass_on(keys.at[SPAN], keys.at[SPAN - 1], 0, 1, 1)
     pass_on(vals.at[SPAN], vals.at[SPAN - 3], 1, 3, 3)
     pass_on(vals.at[SPAN], vals.at[SPAN - 1], 1, 1, 1)
     pass_on(keys.at[SPAN], keys.at[SPAN - 3], 0, 3, 3)
     pass_on(keys.at[SPAN], keys.at[SPAN - 4], 0, 4, 4)
     pass_on(vals.at[SPAN], vals.at[SPAN - 4], 1, 4, 4)
-    with scope("Cr1zx"):
-        share(1, 0)
-        ring(2, relay, 1, "zx")
-    with scope("Cr1y"):
-        ring(2, relay, 1, "y")
+    with scope("query"):
+        share_wait(0, 1)
+        share_wait(0, 2)
+        for p in range(2):
+            raw = jnp.dot(nrm[...], columns(QUERY_AT + 256 * p, 256), preferred_element_type=jnp.float32)
+            for k in range(2):
+                qry[2 * p + k] = rotated(raw[:, k * head : (k + 1) * head]).astype(jnp.bfloat16)
+    share(1, 0)
+
+    def begin_last(g, along):
+        ring(1, both, g, along)
+        ring(2, spread, g, along)
+
+    def advance(g, along):
+        for dim in along:
+            ring(2, relay, g, dim)
+            begin_last(g + 2, dim)
+
+    with scope("Cr1"):
+        ring(2, relay, 1)
     with scope("C2yz"):
-        ring(1, both, 2)
+        ring(1, both, 2, "yz")
         ring(2, spread, 2, "yz")
     with scope("forward"):
         halo_wait(0, 1)
         pass_on(keys.at[SPAN - 1], keys.at[SPAN - 2], 0, 2, 1)
         halo_wait(1, 3)
         pass_on(vals.at[SPAN - 3], vals.at[SPAN - 2], 1, 2, -1)
-    with scope("C2x"):
-        ring(2, spread, 2, "x")
-    with scope("near1"):
-        ring(2, near, 1)
-        share(1, 1, 3)
-    with scope("far1"):
-        ring(2, far, 1)
-        share(1, 2)
-    with scope("F1"):
-        share_wait(1)
-        share(2, 0)
-    with scope("query"):
-        for p in range(2):
-            raw = jnp.dot(nrm[...], columns(QUERY_AT + 256 * p, 256), preferred_element_type=jnp.float32)
-            for k in range(2):
-                qry[2 * p + k] = rotated(raw[:, k * head : (k + 1) * head]).astype(jnp.bfloat16)
-    with scope("halo"):
-        halo_rest(2, 4)
-        halo_rest(0, 3)
-        halo_rest(1, 3)
-
     tall = rows // 2
     scale = math.log2(math.e) / math.sqrt(head)
 
-    def attend(part, h):
-        spans = (
-            [(j, 0, rows) for j in range(SPAN)] + [(SPAN, 0, tall)]
-            if part == 0
-            else [(0, tall, tall)]
-            + [(j, 0, rows) for j in range(1, SPAN)]
-            + [(SPAN, 0, tall), (SPAN, tall, tall)]
-        )
+    def scored(part, h, spans):
         q = qry[h, part * tall : (part + 1) * tall, :]
         own = mine[part * tall : (part + 1) * tall, 0:1]
         scores = []
-        for k, (j, at, n) in enumerate(spans):
+        for j, at, n, causal in spans:
             s = jnp.dot(q, keys[j, :, at : at + n], preferred_element_type=jnp.float32)
             same = marks[j, 0:1, at : at + n] == own
-            if k == len(spans) - 1:
+            if causal:
                 same = same & (
                     lax.broadcasted_iota(jnp.int32, (tall, n), 1)
                     <= lax.broadcasted_iota(jnp.int32, (tall, n), 0)
@@ -362,64 +370,122 @@
         peak = functools.reduce(
             jnp.maximum, [jnp.max(s, axis=1, keepdims=True) for s in scores]
         )
-        total = jnp.zeros((tall, 1), jnp.float32)
-        mixed = jnp.zeros((tall, head), jnp.float32)
-        for (j, at, n), s in zip(spans, scores):
+        return scores, peak
+
+    def weighed(spans, scores, peak, total, mixed):
+        for (j, at, n, _), s in zip(spans, scores):
             e = jnp.exp2((s - peak) * scale)
             total = total + jnp.sum(e, axis=1, keepdims=True)
             mixed = mixed + jnp.dot(
                 e.astype(jnp.bfloat16), vals[j, at : at + n, :], preferred_element_type=jnp.float32
             )
-        att[part * tall : (part + 1) * tall, pl.ds(pl.multiple_of(h * head, head), head)] = (
-            mixed / total
-        ).astype(jnp.bfloat16)
-
-    def attend_heads(part, lo, hi):
+        return total, mixed
+
+    def attend_near(part, h):
+        here = pl.ds(part * tall, tall)
+        spans = [(SPAN, part * tall, tall, True)]
+        if part == 1:
+            spans.append((SPAN, 0, tall, False))
+        spans.append((SPAN - 1, 0, rows, False))
+        scores, peak = scored(part, h, spans)
+        total = jnp.zeros((tall, 1), jnp.float32)
+        mixed = jnp.zeros((tall, head), jnp.float32)
+        total, mixed = weighed(spans, scores, peak, total, mixed)
+        peaks[h, here, :] = jnp.broadcast_to(peak, (tall, head))
+        sums[h, here, :] = jnp.broadcast_to(total, (tall, head))
+        mixes[h, here, :] = mixed
+
+    def attend_far(part, h):
+        here = pl.ds(part * tall, tall)
+        spans = [(0, tall * part, rows - tall * part, False)]
+        spans += [(j, 0, rows, False) for j in range(1, SPAN - 1)]
+        scores, peak = scored(part, h, spans)
+        old = peaks[h, here, 0:1]
+        peak = jnp.maximum(peak, old)
+        factor = jnp.exp2((old - peak) * scale)
+        total = sums[h, here, 0:1] * factor
+        mixed = mixes[h, here, :] * factor
+        total, mixed = weighed(spans, scores, peak, total, mixed)
+        att[here, pl.ds(pl.multiple_of(h * head, head), head)] = (mixed / total).astype(jnp.bfloat16)
+
+    def attend_heads(what, part, lo, hi):
         def step(h, carry):
-            attend(part, h)
+            what(part, h)
             return carry
 
         lax.fori_loop(lo, hi, step, 0)
 
+    with scope("C2x"):
+        begin_last(2, "x")
+    with scope("C3"):
+        begin_last(3, "yzx")
+    with scope("near1"):
+        ring(2, near, 1)
+        share(1, 1, 3)
+    with scope("early0"):
+        halo_rest(2, 4)
+        halo_wait(1, 1)
+        attend_heads(attend_near, 0, 0, heads)
+    with scope("early1"):
+        attend_heads(attend_near, 1, 0, heads)
+    with scope("Cr2y"):
+        advance(2, "y")
+    with scope("far1"):
+        ring(2, far, 1)
+        share(1, 2)
+    with scope("halo"):
+        halo_rest(0, 3)
+        halo_rest(1, 2)
     with scope("attend0"):
-        attend_heads(0, 0, 2)
-    with scope("Cr2"):
-        ring(2, relay, 2)
-    with scope("C3"):
-        ring(1, both, 3)
-        ring(2, spread, 3)
+        attend_heads(attend_far, 0, 0, 2)
+    with scope("Cr2zx"):
+        advance(2, "zx")
+
+    share(2, 0)
     with scope("attend1"):
-        attend_heads(0, 2, 4)
+        attend_heads(attend_far, 0, 2, 4)
+    with scope("Cr3y"):
+        advance(3, "y")
     with scope("attend2"):
-        attend_heads(1, 0, 2)
+        attend_heads(attend_far, 1, 0, 2)
     with scope("near2"):
         ring(2, near, 2)
         share(2, 1, 3)
-        share(3, 0)
     with scope("attend3"):
-        attend_heads(1, 2, 4)
-
-    def wide_step(lhs, at, n, after, squares=False):
+        attend_heads(attend_far, 1, 2, 4)
+    share(3, 0)
+    with scope("Cr3xz"):
+        advance(3, "xz")
+    with scope("F1"):
+        share_wait(1)
+
+    def wide_step(lhs, lo, n, at, use):
         per = 2 * 2 * SIDE * shard
 
         def step(k, carry):
             for zz in range(2):
                 rhs = w[k, 2 * zz : 2 * zz + 2, :, :, :, at : at + n].reshape(per, n)
                 got = lax.dot_general(
-                    lhs[...], rhs, (((1,), (1,)), ((), ())), preferred_element_type=jnp.float32
+                    lhs[:, lo : lo + n], rhs, (((1,), (1,)), ((), ())), preferred_element_type=jnp.float32
                 )
-                here = pl.ds(pl.multiple_of((k * 2 + zz) * per, per), per)
-                new = (res[:, here].astype(jnp.float32) + got).astype(jnp.bfloat16)
-                res[:, here] = new
-                if squares:
-                    wide = new.astype(jnp.float32)
-                    wide = wide * wide
-                    sums = [wide[:, i * head : (i + 1) * head] for i in range(per // head)]
-                    power[...] += functools.reduce(jnp.add, sums)
-            after(k)
+                use(pl.ds(pl.multiple_of((k * 2 + zz) * per, per), per), got)
             return carry
 
         lax.fori_loop(0, SIDE, step, 0)
+
+    def project(here, got):
+        new = (res[:, here].astype(jnp.float32) + got).astype(jnp.bfloat16)
+        res[:, here] = new
+        wide = new.astype(jnp.float32)
+        wide = wide * wide
+        parts = [wide[:, i * head : (i + 1) * head] for i in range(got.shape[1] // head)]
+        power[...] += functools.reduce(jnp.add, parts)
+
+    def begin(here, got):
+        acc[:, here] = res[:, here].astype(jnp.float32) + got
+
+    def end(here, got):
+        res[:, here] = (acc[:, here] + got).astype(jnp.bfloat16)
 
     def scaled(gain):
         mean = jnp.sum(power[...], axis=-1, keepdims=True) / width
@@ -438,48 +504,71 @@
 
     power[...] = jnp.zeros_like(power)
     with scope("project"):
-        wide_step(att, OUT_AT, 512, lambda k: None, squares=True)
+        wide_step(att, 0, heads * head, OUT_AT, project)
     with scope("far2"):
         ring(2, far, 2)
         share(2, 2)
     with scope("mlp_norm"):
         scaled(gain_mlp)
-    with scope("Cr3"):
-        ring(2, relay, 3)
     with scope("F2"):
         share_wait(2)
 
-    def gated(lo, hi):
-        def step(j, carry):
-            at = pl.multiple_of(j * 256, 256)
-            gate = jnp.dot(nrm[...], columns(GATE_AT + at, 256), preferred_element_type=jnp.float32)
-            up = jnp.dot(nrm[...], columns(UP_AT + at, 256), preferred_element_type=jnp.float32)
-            hid[:, pl.ds(at, 256)] = (gate / (1.0 + jnp.exp(-gate)) * up).astype(jnp.bfloat16)
-            return carry
-
-        lax.fori_loop(lo, hi, step, 0)
-
-    with scope("gated0"):
-        gated(0, 2)
+    def gated(part, j):
+        at = 256 * j
+        gate = jnp.dot(nrm[...], columns(GATE_AT[part] + at, 256), preferred_element_type=jnp.float32)
+        up = jnp.dot(nrm[...], columns(UP_AT[part] + at, 256), preferred_element_type=jnp.float32)
+        here = part * some + at
+        hid[:, here : here + 256] = (gate / (1.0 + jnp.exp(-gate)) * up).astype(jnp.bfloat16)
+
+    with scope("Cr4"):
+        ring(2, relay, 4)
     with scope("near3"):
         ring(2, near, 3)
         share(3, 1, 3)
+    with scope("gated0"):
+        gated(0, 0)
     with scope("gated1"):
-        gated(2, 4)
-    with scope("F3"):
+        gated(0, 1)
+    with scope("far3"):
         ring(2, far, 3)
         share(3, 2)
+        share(4, 0)
+    with scope("F3"):
         share_wait(3)
-
-    with scope("down"):
-        wide_step(hid, DOWN_AT, 1024, lambda k: None)
+    with scope("near4"):
+        ring(2, near, 4)
+        share(4, 1, 3)
+    with scope("Cr5"):
+        ring(2, relay, 5)
+    with scope("gated2"):
+        gated(1, 0)
+    with scope("far4"):
+        ring(2, far, 4)
+        share(4, 2)
+        share(5, 0)
+    with scope("gated3"):
+        gated(1, 1)
+    with scope("near5"):
+        ring(2, near, 5)
+        share(5, 1, 3)
+    with scope("far5"):
+        ring(2, far, 5)
+        share(5, 2)
+    with scope("F4"):
+        share_wait(4)
+    with scope("down0"):
+        wide_step(hid, 0, LAST, DOWN_AT, begin)
+    with scope("F5"):
+        share_wait(5)
+    with scope("down1"):
+        wide_step(hid, LAST, hid.shape[1] - LAST, DOWN_AT + LAST, end)
     assert len(arrivals) <= ARRIVALS
     with scope("sent"):
         three = pl.ds(0, 3)
         for k, ref in enumerate(
             (w.at[0, 0, 0, three], w.at[0, three, 0], w.at[three, ALL, 0], w.at[ALL, ALL, 0])
         ):
-            remote(ref, ("share", 0), device(pos, 1 - c), k).wait_send()
+            remote(ref, shared(0, 1), device(pos, 1 - c), k).wait_send()
         for slot, buf in enumerate((keys, vals, marks)):
             ref = buf.at[pl.ds(0, 4)]
             halo(ref, ref, slot, 4, 4).wait_send()
@@ -513,8 +602,12 @@
             pltpu.VMEM((rows, head), jnp.float32),
             pltpu.VMEM((rows, head), jnp.float32),
             pltpu.VMEM((rows, head), jnp.float32),
+            pltpu.VMEM((heads, rows, head), jnp.float32),
+            pltpu.VMEM((heads, rows, head), jnp.float32),
+            pltpu.VMEM((heads, rows, head), jnp.float32),
             pltpu.VMEM((rows, heads * head), bf16),
             pltpu.VMEM((rows, w_gate.shape[1]), bf16),
+            pltpu.VMEM((rows, width), jnp.float32),
             pltpu.SemaphoreType.DMA((7,)),
             pltpu.SemaphoreType.DMA((ARRIVALS,)),
             pltpu.SemaphoreType.DMA((1,)),

time: 101 us -> 97.7 us (0.967)
  Pallas kernels: 98.3 us -> 95.6 us
    pallas_call x1, Pallas kernels: 98.3 us -> 95.6 us  [per_device(): pl.pallas_call(kernel, out_shape=pltpu.VMEM((rows, width), bf16), in_spec...]
where the time goes in v3:
time: 97.7 us; the launch traced here: 97.6 us
  Pallas kernels  95.6 us (98%)
  local copies, waits for them, and re-layouts  2.02 us (2%)
    pallas_call x1, Pallas kernels, per_device(): pl.pallas_call(kernel, out_shape=pltpu.VMEM((rows, width), bf16), in_spec...  95.6 us
    unnamed x1, local copies, waits for them, and re-layouts  2.02 us

profile of v3, /device:TPU:1, one launch (start us, length us, event | category | flops | bytes accessed | tf_op | source)
XLA Modules:
  0.0 97.6 jit_solution(267722980636409792)
XLA Ops:
  0.0 95.6 %shard_map.109 = bf16[512,4096]{1,0:T(8,128)(2,1)S(1)} custom-call(bf16[512,4096]{1,0:T(8,128)(2,1)} %tok.1, f32[1,4096]{1,0:T(1,128)} %bitcast.7, f32[1,4096]{1,0:T(1,128)} %bitcast.8, f32[1,128]{1,0:T(1,128)} %constant.2.clone.freqs, s32[1,512]{1,0:T(1,128)} %bitcast.9, bf16[32,512]{1,0:T(8,128)(2,1)} %wq.1, bf16[32,256]{1,0:T(8,128)(2,1)} %wkv.1, ...), custom_call_target="tpu_custom_call" | custom-call | tf_op jit(solution)/shard_map/pallas_call | solution.py:589
  95.6 2.0 %copy.13 = bf16[512,4096]{1,0:T(8,128)(2,1)} copy(bf16[512,4096]{1,0:T(8,128)(2,1)S(1)} %shard_map.109) | data formatting | bytes 8388608
